TPU v7x, 32 devices: a whole 2x2x4 slice. The times are simulated.
32 devices in a mesh: groups: 2 (over y), dom: 8 (over z, core), tilt: 2 (over x), rep: 1.
Axes of the slice: x: 2, y: 2, z: 4, core: 2. Of those that a mesh axis runs over, the one named last changes fastest.
Arguments:
- patches: bfloat16 [4, 1024, 128, 128], P(('groups', 'tilt'), 'dom'), parts along dimension 0, may hold values from -6 to 6
- slot_view: int32 [4, 1024, 1], P(('groups', 'tilt'), 'dom'), parts along dimension 0, may hold values from 0 to 31, as said below
- slot_tilt: int32 [4, 1024], P(('groups', 'tilt'), 'dom'), parts along dimension 0, may hold values from 0 to 9
- slot_pos: bfloat16 [2, 4, 1024], P(None, ('groups', 'tilt'), 'dom'), parts along dimension 1, may hold values from 0 to 1
- defocus: bfloat16 [4, 1024], P(('groups', 'tilt'), 'dom'), parts along dimension 0, may hold values from 1 to 3
- projections: bfloat16 [64, 20, 2, 128, 128], P(('groups', 'dom'), 'tilt', None, 'rep'), parts along dimension 0, may hold values from -6 to 6
- warp_grid: float32 [40, 2, 256], P(('groups', 'tilt')), parts along dimension 0, may hold values from -6 to 6
Outputs:
- slot_terms: float32 [3, 4, 1024], P(None, ('groups', 'tilt'), 'dom'), parts along dimension 1
- new_warp: float32 [40, 2, 256], P(('groups', 'tilt')), parts along dimension 0
There are 2 independent parts, one for each index of `groups`. A program takes and returns all parts, laid end to end along the dimension named above; each array names one. Nothing has to cross between parts.
Inputs may be any that keep to these rules, and one draw needn't show every extreme that they name: `slot_view`: view v is owned by dom index v // 4. Among the 128 slots of one device (one tilt index and one dom index) at most 24 name views of any one owner, and in every such block some owner is named exactly 24 times.
All inputs are finite; a program needn't handle non-finite values.
Results may differ from a plain program's by a relative error of at most 0.0018.
Values may be sent and summed in bfloat16 or wider, within the bound.
A program may use at most 64 MiB of HBM per device.

v0:
```python
import math
import jax
import jax.numpy as jnp
from jax import lax
from jax.sharding import PartitionSpec as P

GRID = 16
AMPLITUDE = 0.07
TRUST_FLOOR = 0.02


def signed_freq(index, pixels):
    return jnp.where(index < pixels // 2, index, index - pixels).astype(jnp.float32)


def dft_tables(freq_rows, pixels):
    columns = jnp.arange(pixels, dtype=jnp.int32)
    table_scale = 1.0 / math.sqrt(pixels)
    turns_rows = (freq_rows[:, None] * columns[None, :] % pixels).astype(jnp.float32) * (
        2.0 * math.pi / pixels
    )
    turns_full = (columns[:, None] * columns[None, :] % pixels).astype(jnp.float32) * (
        2.0 * math.pi / pixels
    )
    row_table = jnp.concatenate([jnp.cos(turns_rows), jnp.sin(turns_rows)], axis=0) * table_scale
    col_table = jnp.concatenate([jnp.cos(turns_full), jnp.sin(turns_full)], axis=1) * table_scale
    return (row_table.astype(jnp.bfloat16), col_table.astype(jnp.bfloat16))


def node_weights(pos_x, pos_y, grid_side):
    knot_pos = jnp.arange(grid_side, dtype=jnp.int32).astype(jnp.float32)
    weight_x = jnp.maximum(0.0, 1.0 - jnp.abs(pos_x[:, None] * (grid_side - 1) - knot_pos[None, :]))
    weight_y = jnp.maximum(0.0, 1.0 - jnp.abs(pos_y[:, None] * (grid_side - 1) - knot_pos[None, :]))
    return (weight_y[:, :, None] * weight_x[:, None, :]).reshape(
        pos_x.shape[0], grid_side * grid_side
    )


def spectral_terms(spectrum, ref_blk, focus_blk, shift_blk, freq_rows, pixels):
    row_total = freq_rows.shape[0]
    v_one_cos = spectrum[:, :row_total, :pixels]
    v_one_sin = spectrum[:, :row_total, pixels:]
    v_two_cos = spectrum[:, row_total:, :pixels]
    v_two_sin = spectrum[:, row_total:, pixels:]
    real_part = v_one_cos - v_two_sin
    imag_part = -(v_one_sin + v_two_cos)
    freq_y = signed_freq(freq_rows, pixels)[None, :, None]
    freq_x = signed_freq(jnp.arange(pixels, dtype=jnp.int32), pixels)[None, None, :]
    nyquist = pixels / 2.0
    radius = (freq_y * freq_y + freq_x * freq_x) / (nyquist * nyquist)
    aberration = math.pi * focus_blk[:, None, None] * radius
    contrast = -(
        math.sqrt(1.0 - AMPLITUDE * AMPLITUDE) * jnp.sin(aberration)
        + AMPLITUDE * jnp.cos(aberration)
    )
    phase_angle = (
        2.0
        * math.pi
        / pixels
        * (freq_x * shift_blk[:, 0, None, None] + freq_y * shift_blk[:, 1, None, None])
    )
    cosine = jnp.cos(phase_angle)
    sine_part = jnp.sin(phase_angle)
    ref_real = ref_blk[:, 0].astype(jnp.float32)
    ref_imag = ref_blk[:, 1].astype(jnp.float32)
    model_real = contrast * (ref_real * cosine + ref_imag * sine_part)
    model_imag = contrast * (ref_imag * cosine - ref_real * sine_part)
    diff_real = real_part - model_real
    diff_imag = imag_part - model_imag
    inverse_area = 1.0 / (pixels * pixels)
    energy = jnp.sum(diff_real * diff_real + diff_imag * diff_imag, axis=(1, 2)) * inverse_area
    cross_term = diff_imag * model_real - diff_real * model_imag
    grad_x = 2.0 * inverse_area * jnp.sum(2.0 * math.pi / pixels * freq_x * cross_term, axis=(1, 2))
    grad_y = 2.0 * inverse_area * jnp.sum(2.0 * math.pi / pixels * freq_y * cross_term, axis=(1, 2))
    return jnp.stack([energy, grad_x, grad_y], axis=1)


def on_device(patches, slot_view, slot_tilt, slot_pos, defocus, projections, warp_grid):
    owners = lax.axis_size("dom")
    slot_count = patches.shape[1]
    pixels = patches.shape[-1]
    view_dev = projections.shape[0]
    tilt_dev = warp_grid.shape[0]
    node_count = warp_grid.shape[2]
    capacity = 3 * slot_count // (2 * owners)
    buffer_len = owners * capacity
    chosen_view = slot_view[0, :, 0]
    owner_of = chosen_view // view_dev
    owner_hits = (owner_of[:, None] == jnp.arange(owners, dtype=jnp.int32)[None, :]).astype(
        jnp.int32
    )
    earlier = jnp.cumsum(owner_hits, axis=0) - owner_hits
    slot_rank = jnp.sum(earlier * owner_hits, axis=1)
    target = owner_of * capacity + slot_rank
    matches = target[None, :] == jnp.arange(buffer_len, dtype=jnp.int32)[:, None]
    source = jnp.sum(
        jnp.where(matches, jnp.arange(slot_count, dtype=jnp.int32)[None, :], 0), axis=1
    )
    filled = jnp.any(matches, axis=1)
    patch_rows = jnp.where(filled[:, None, None], patches[0][source], jnp.zeros((), jnp.bfloat16))
    slot_meta = jnp.stack(
        [
            slot_tilt[0].astype(jnp.float32),
            (chosen_view % view_dev).astype(jnp.float32),
            defocus[0].astype(jnp.float32),
            slot_pos[0, 0].astype(jnp.float32),
            slot_pos[1, 0].astype(jnp.float32),
            jnp.ones((slot_count,), jnp.float32),
        ],
        axis=1,
    )
    meta_rows = jnp.where(filled[:, None], slot_meta[source], 0.0).astype(jnp.bfloat16)
    patch_buffer = patch_rows.reshape(owners, capacity, pixels, pixels)
    meta_buffer = meta_rows.reshape(owners, capacity, 6)
    row_span = projections.shape[3]
    freq_rows = lax.axis_index("rep") * row_span + jnp.arange(row_span, dtype=jnp.int32)
    row_table, col_table = dft_tables(freq_rows, pixels)
    row_total = freq_rows.shape[0]
    projected_flat = projections.reshape(view_dev * tilt_dev, 2, row_total, pixels)
    tilt_iota = jnp.arange(tilt_dev, dtype=jnp.int32)
    view_iota = jnp.arange(view_dev, dtype=jnp.int32)

    def one_block(inputs):
        patch_blk, index_blk, focus_blk, shift_blk = inputs
        ref_blk = projected_flat[index_blk]
        first_pass = jnp.einsum(
            "fy,byx->bfx", row_table, patch_blk, preferred_element_type=jnp.float32
        ).astype(jnp.bfloat16)
        spectrum = jnp.einsum(
            "bfx,xk->bfk", first_pass, col_table, preferred_element_type=jnp.float32
        )
        return spectral_terms(spectrum, ref_blk, focus_blk, shift_blk, freq_rows, pixels)

    patch_in = lax.all_to_all(patch_buffer, "dom", split_axis=0, concat_axis=0, tiled=True)
    meta_in = lax.all_to_all(meta_buffer, "dom", split_axis=0, concat_axis=0, tiled=True)
    senders = patch_in.shape[0]
    per_sender = patch_in.shape[1]
    slot_total = senders * per_sender
    meta_flat = meta_in.reshape(slot_total, 6).astype(jnp.float32)
    tilt_match = meta_flat[:, 0:1] == tilt_iota.astype(jnp.float32)[None, :]
    view_match = meta_flat[:, 1:2] == view_iota.astype(jnp.float32)[None, :]
    tilt_local = jnp.sum(jnp.where(tilt_match, tilt_iota[None, :], 0), axis=1)
    view_local = jnp.sum(jnp.where(view_match, view_iota[None, :], 0), axis=1)
    weights = node_weights(meta_flat[:, 3], meta_flat[:, 4], GRID)
    shifts = jnp.sum(warp_grid[tilt_local] * weights[:, None, :], axis=2)
    block_len = math.gcd(slot_total, 16)
    block_count = slot_total // block_len
    per_slot = lax.map(
        one_block,
        (
            patch_in.reshape(block_count, block_len, pixels, pixels),
            (view_local * tilt_dev + tilt_local).reshape(block_count, block_len),
            meta_flat[:, 2].reshape(block_count, block_len),
            shifts.reshape(block_count, block_len, 2),
        ),
    ).reshape(slot_total, 3)
    node_coef = (
        tilt_match.astype(jnp.float32)[:, :, None]
        * per_slot[:, None, 1:3]
        * meta_flat[:, 5, None, None]
    ).reshape(senders, per_sender, 2 * tilt_dev)
    returned = lax.all_to_all(
        per_slot.reshape(senders, per_sender, 3), "dom", split_axis=0, concat_axis=0, tiled=True
    )
    weight_all = weights.reshape(senders, per_sender, node_count)
    own_terms = returned.reshape(buffer_len, 3)[target]
    summed = lax.psum(own_terms, "rep")
    slot_terms = summed.T[:, None, :]
    gradient = jnp.dot(
        node_coef.reshape(-1, 2 * tilt_dev).T,
        weight_all.reshape(-1, node_count),
        precision=lax.Precision.HIGHEST,
        preferred_element_type=jnp.float32,
    ).reshape(tilt_dev, 2, node_count)
    whole_grad = lax.psum(gradient, ("dom", "rep"))
    new_warp = warp_grid - whole_grad / jnp.sqrt(
        whole_grad * whole_grad + TRUST_FLOOR * TRUST_FLOOR
    )
    return (slot_terms, new_warp)


def solution(mesh):
    in_specs = (
        P(("groups", "tilt"), "dom", None, None),
        P(("groups", "tilt"), "dom", None),
        P(("groups", "tilt"), "dom"),
        P(None, ("groups", "tilt"), "dom"),
        P(("groups", "tilt"), "dom"),
        P(("groups", "dom"), "tilt", None, "rep", None),
        P(("groups", "tilt"), None, None),
    )
    out_specs = (P(None, ("groups", "tilt"), "dom"), P(("groups", "tilt"), None, None))
    return jax.shard_map(
        on_device, mesh=mesh, in_specs=in_specs, out_specs=out_specs, check_vma=False
    )
```

profile of v0, /device:TPU:0, one launch (start us, length us, event | category | flops | bytes accessed | tf_op | source)
XLA Modules:
  0.0 444.6 jit_solution(1007006649997248516)
XLA Ops:
  0.6 0.7 and_select_fusion.2
  1.7 0.7 fusion.48
  2.4 0.7 multiply_add_fusion.1
  3.3 0.7 bitcast_convert_fusion
  4.1 0.7 convert_bitcast_fusion
  4.7 0.7 stack.8
  5.6 0.8 gather_fusion.2
  6.5 0.6 select_convert_fusion
  7.2 6.4 %all-to-all-start.1 = ((bf16[8,24,6]{1,2,0:T(8,128)(2,1)}), bf16[8,24,6]{1,2,0:T(8,128)(2,1)S(1)}, u32[]{:S(2)}, u32[]{:S(2)}) async-start(bf16[8,24,6]{1,2,0:T(8,128)(2,1)} %select_convert_fusion), calls=%async_computation.1 | async-start | bytes 32768 | tf_op jit(solution)/shard_map/all_to_all | solution.py:135
  13.5 10.2 %gather_fusion.1 = bf16[192,128,128]{2,1,0:T(8,128)(2,1)} fusion(bf16[128,128,128]{2,1,0:T(8,128)(2,1)} %bitcast.181, s32[1024]{0:T(1024)S(1)} %pad_clamp_fusion.3), kind=kCustom, calls=%fused_computation.1 | custom fusion | bytes 12583680 | tf_op jit(solution)/shard_map/gather | solution.py:100
  23.8 8.6 %copy.103 = bf16[8,24,128,128]{2,3,1,0:T(8,128)(2,1)} copy(bf16[8,24,128,128]{3,2,1,0:T(8,128)(2,1)} %bitcast.179) | data formatting | bytes 12582912 | tf_op jit(solution)/shard_map/gather | solution.py:100
  32.4 5.9 %broadcast_select_fusion = bf16[8,24,128,128]{2,3,1,0:T(8,128)(2,1)} fusion(bf16[8,24,128,128]{2,3,1,0:T(8,128)(2,1)} %copy.103, pred[8,24]{1,0:T(8,128)(4,1)S(1)} %broadcast_in_dim.106), kind=kLoop, calls=%fused_computation.65 | loop fusion | flops 3145728 | bytes 12583104 | tf_op jit(solution)/shard_map/jit(_where)/select_n | solution.py:100
  38.3 5.2 %all-to-all-start = ((bf16[8,24,128,128]{2,3,1,0:T(8,128)(2,1)}), bf16[8,24,128,128]{2,3,1,0:T(8,128)(2,1)}, u32[]{:S(2)}, u32[]{:S(2)}) async-start(bf16[8,24,128,128]{2,3,1,0:T(8,128)(2,1)} %broadcast_select_fusion), calls=%async_computation | async-start | bytes 12582912 | tf_op jit(solution)/shard_map/all_to_all | solution.py:134
  44.4 1.1 gather_fusion.3
  46.3 136.3 %all-to-all-done = bf16[8,24,128,128]{2,3,1,0:T(8,128)(2,1)} async-done(((bf16[8,24,128,128]{2,3,1,0:T(8,128)(2,1)}), bf16[8,24,128,128]{2,3,1,0:T(8,128)(2,1)}, u32[]{:S(2)}, u32[]{:S(2)}) %all-to-all-start) | async-done | bytes 6291488 | tf_op jit(solution)/shard_map/all_to_all | solution.py:134
  182.6 223.7 %while.15 = (s32[]{:T(128)}, f32[12,16,3]{1,0,2:T(8,128)S(1)}, bf16[12,16,128,128]{2,3,1,0:T(8,128)(2,1)}, bf16[256,128]{1,0:T(8,128)(2,1)S(1)}, bf16[128,256]{1...) while((s32[]{:T(128)}, f32[12,16,3]{1,0,2:T(8,128)S(1)}, ...), condition=%wide.region_11.12_spmd.clone.clone, body=%wide.region_7.11_spmd.clone.clone.sunk | while | flops 411868064 | bytes 14461309 | solution.py:148
  182.7 4.5 %fusion.62 = f32[16,256,256]{2,1,0:T(8,128)} fusion(bf16[12,16,128,128]{2,3,1,0:T(8,128)(2,1)} %get-tuple-element.403, s32[]{:T(128)} %get-tuple-element.390, bf16[128,256]{1,0:T(8,128)(2,1)S(1)} %get-tuple-element.405, bf16[256,128]{1,0:T(8,128)(2,1)S(1)} %get-tuple-element.404), kind=kOutput, calls=%fused_computation.10.clone.1 | convolution fusion | flops 403177472 | bytes 4850176 | tf_op jit(solution)/shard_map/while/body/eval_jaxpr/bfx,xk->bfk/dot_general | solution.py:129
  187.2 2.5 gather_fusion
  189.8 10.9 %add_reduce_fusion.2 = (f32[16]{0:T(128)S(1)}, f32[16,128,128]{2,1,0:T(8,128)S(1)}) fusion(f32[16,256,256]{2,1,0:T(8,128)} %fusion.62, bf16[16,2,128,128]{3,2,1,0:T(8,128)(2,1)S(1)} %gather_fusion, f32[16,128]{1,0:T(8,128)S(1)} %get-tuple-element.371, f32[16,128]{1,0:T(8,128)S(1)} %get-tuple-element.372, f32[128,128]{1,0:T(8,128)S(1)} %add_multiply_fusion.3, ...), kind=kLoop, calls=%fused_computation.31.clone.1 | loop fusion | flops 7602160 | bytes 6373504 | tf_op jit(solution)/shard_map/while/body/eval_jaxpr/reduce_sum | solution.py:71
  200.8 0.3 multiply_reduce_fusion.4
  201.3 4.5 %fusion.62 = f32[16,256,256]{2,1,0:T(8,128)} fusion(bf16[12,16,128,128]{2,3,1,0:T(8,128)(2,1)} %get-tuple-element.403, s32[]{:T(128)} %get-tuple-element.390, bf16[128,256]{1,0:T(8,128)(2,1)S(1)} %get-tuple-element.405, bf16[256,128]{1,0:T(8,128)(2,1)S(1)} %get-tuple-element.404), kind=kOutput, calls=%fused_computation.10.clone.1 | convolution fusion | flops 403177472 | bytes 4850176 | tf_op jit(solution)/shard_map/while/body/eval_jaxpr/bfx,xk->bfk/dot_general | solution.py:129
  205.9 2.5 gather_fusion
  208.5 10.9 %add_reduce_fusion.2 = (f32[16]{0:T(128)S(1)}, f32[16,128,128]{2,1,0:T(8,128)S(1)}) fusion(f32[16,256,256]{2,1,0:T(8,128)} %fusion.62, bf16[16,2,128,128]{3,2,1,0:T(8,128)(2,1)S(1)} %gather_fusion, f32[16,128]{1,0:T(8,128)S(1)} %get-tuple-element.371, f32[16,128]{1,0:T(8,128)S(1)} %get-tuple-element.372, f32[128,128]{1,0:T(8,128)S(1)} %add_multiply_fusion.3, ...), kind=kLoop, calls=%fused_computation.31.clone.1 | loop fusion | flops 7602160 | bytes 6373504 | tf_op jit(solution)/shard_map/while/body/eval_jaxpr/reduce_sum | solution.py:71
  219.4 0.3 multiply_reduce_fusion.4
  220.0 4.5 %fusion.62 = f32[16,256,256]{2,1,0:T(8,128)} fusion(bf16[12,16,128,128]{2,3,1,0:T(8,128)(2,1)} %get-tuple-element.403, s32[]{:T(128)} %get-tuple-element.390, bf16[128,256]{1,0:T(8,128)(2,1)S(1)} %get-tuple-element.405, bf16[256,128]{1,0:T(8,128)(2,1)S(1)} %get-tuple-element.404), kind=kOutput, calls=%fused_computation.10.clone.1 | convolution fusion | flops 403177472 | bytes 4850176 | tf_op jit(solution)/shard_map/while/body/eval_jaxpr/bfx,xk->bfk/dot_general | solution.py:129
  224.5 2.5 gather_fusion
  227.1 10.9 %add_reduce_fusion.2 = (f32[16]{0:T(128)S(1)}, f32[16,128,128]{2,1,0:T(8,128)S(1)}) fusion(f32[16,256,256]{2,1,0:T(8,128)} %fusion.62, bf16[16,2,128,128]{3,2,1,0:T(8,128)(2,1)S(1)} %gather_fusion, f32[16,128]{1,0:T(8,128)S(1)} %get-tuple-element.371, f32[16,128]{1,0:T(8,128)S(1)} %get-tuple-element.372, f32[128,128]{1,0:T(8,128)S(1)} %add_multiply_fusion.3, ...), kind=kLoop, calls=%fused_computation.31.clone.1 | loop fusion | flops 7602160 | bytes 6373504 | tf_op jit(solution)/shard_map/while/body/eval_jaxpr/reduce_sum | solution.py:71
  238.1 0.3 multiply_reduce_fusion.4
  238.6 4.5 %fusion.62 = f32[16,256,256]{2,1,0:T(8,128)} fusion(bf16[12,16,128,128]{2,3,1,0:T(8,128)(2,1)} %get-tuple-element.403, s32[]{:T(128)} %get-tuple-element.390, bf16[128,256]{1,0:T(8,128)(2,1)S(1)} %get-tuple-element.405, bf16[256,128]{1,0:T(8,128)(2,1)S(1)} %get-tuple-element.404), kind=kOutput, calls=%fused_computation.10.clone.1 | convolution fusion | flops 403177472 | bytes 4850176 | tf_op jit(solution)/shard_map/while/body/eval_jaxpr/bfx,xk->bfk/dot_general | solution.py:129
  243.2 2.5 gather_fusion
  245.8 10.9 %add_reduce_fusion.2 = (f32[16]{0:T(128)S(1)}, f32[16,128,128]{2,1,0:T(8,128)S(1)}) fusion(f32[16,256,256]{2,1,0:T(8,128)} %fusion.62, bf16[16,2,128,128]{3,2,1,0:T(8,128)(2,1)S(1)} %gather_fusion, f32[16,128]{1,0:T(8,128)S(1)} %get-tuple-element.371, f32[16,128]{1,0:T(8,128)S(1)} %get-tuple-element.372, f32[128,128]{1,0:T(8,128)S(1)} %add_multiply_fusion.3, ...), kind=kLoop, calls=%fused_computation.31.clone.1 | loop fusion | flops 7602160 | bytes 6373504 | tf_op jit(solution)/shard_map/while/body/eval_jaxpr/reduce_sum | solution.py:71
  256.7 0.3 multiply_reduce_fusion.4
  257.3 4.5 %fusion.62 = f32[16,256,256]{2,1,0:T(8,128)} fusion(bf16[12,16,128,128]{2,3,1,0:T(8,128)(2,1)} %get-tuple-element.403, s32[]{:T(128)} %get-tuple-element.390, bf16[128,256]{1,0:T(8,128)(2,1)S(1)} %get-tuple-element.405, bf16[256,128]{1,0:T(8,128)(2,1)S(1)} %get-tuple-element.404), kind=kOutput, calls=%fused_computation.10.clone.1 | convolution fusion | flops 403177472 | bytes 4850176 | tf_op jit(solution)/shard_map/while/body/eval_jaxpr/bfx,xk->bfk/dot_general | solution.py:129
  261.8 2.5 gather_fusion
  264.4 10.9 %add_reduce_fusion.2 = (f32[16]{0:T(128)S(1)}, f32[16,128,128]{2,1,0:T(8,128)S(1)}) fusion(f32[16,256,256]{2,1,0:T(8,128)} %fusion.62, bf16[16,2,128,128]{3,2,1,0:T(8,128)(2,1)S(1)} %gather_fusion, f32[16,128]{1,0:T(8,128)S(1)} %get-tuple-element.371, f32[16,128]{1,0:T(8,128)S(1)} %get-tuple-element.372, f32[128,128]{1,0:T(8,128)S(1)} %add_multiply_fusion.3, ...), kind=kLoop, calls=%fused_computation.31.clone.1 | loop fusion | flops 7602160 | bytes 6373504 | tf_op jit(solution)/shard_map/while/body/eval_jaxpr/reduce_sum | solution.py:71
  275.9 4.5 %fusion.62 = f32[16,256,256]{2,1,0:T(8,128)} fusion(bf16[12,16,128,128]{2,3,1,0:T(8,128)(2,1)} %get-tuple-element.403, s32[]{:T(128)} %get-tuple-element.390, bf16[128,256]{1,0:T(8,128)(2,1)S(1)} %get-tuple-element.405, bf16[256,128]{1,0:T(8,128)(2,1)S(1)} %get-tuple-element.404), kind=kOutput, calls=%fused_computation.10.clone.1 | convolution fusion | flops 403177472 | bytes 4850176 | tf_op jit(solution)/shard_map/while/body/eval_jaxpr/bfx,xk->bfk/dot_general | solution.py:129
  280.5 2.5 gather_fusion
  283.1 10.9 %add_reduce_fusion.2 = (f32[16]{0:T(128)S(1)}, f32[16,128,128]{2,1,0:T(8,128)S(1)}) fusion(f32[16,256,256]{2,1,0:T(8,128)} %fusion.62, bf16[16,2,128,128]{3,2,1,0:T(8,128)(2,1)S(1)} %gather_fusion, f32[16,128]{1,0:T(8,128)S(1)} %get-tuple-element.371, f32[16,128]{1,0:T(8,128)S(1)} %get-tuple-element.372, f32[128,128]{1,0:T(8,128)S(1)} %add_multiply_fusion.3, ...), kind=kLoop, calls=%fused_computation.31.clone.1 | loop fusion | flops 7602160 | bytes 6373504 | tf_op jit(solution)/shard_map/while/body/eval_jaxpr/reduce_sum | solution.py:71
  294.6 4.5 %fusion.62 = f32[16,256,256]{2,1,0:T(8,128)} fusion(bf16[12,16,128,128]{2,3,1,0:T(8,128)(2,1)} %get-tuple-element.403, s32[]{:T(128)} %get-tuple-element.390, bf16[128,256]{1,0:T(8,128)(2,1)S(1)} %get-tuple-element.405, bf16[256,128]{1,0:T(8,128)(2,1)S(1)} %get-tuple-element.404), kind=kOutput, calls=%fused_computation.10.clone.1 | convolution fusion | flops 403177472 | bytes 4850176 | tf_op jit(solution)/shard_map/while/body/eval_jaxpr/bfx,xk->bfk/dot_general | solution.py:129
  299.1 2.5 gather_fusion
  301.7 10.9 %add_reduce_fusion.2 = (f32[16]{0:T(128)S(1)}, f32[16,128,128]{2,1,0:T(8,128)S(1)}) fusion(f32[16,256,256]{2,1,0:T(8,128)} %fusion.62, bf16[16,2,128,128]{3,2,1,0:T(8,128)(2,1)S(1)} %gather_fusion, f32[16,128]{1,0:T(8,128)S(1)} %get-tuple-element.371, f32[16,128]{1,0:T(8,128)S(1)} %get-tuple-element.372, f32[128,128]{1,0:T(8,128)S(1)} %add_multiply_fusion.3, ...), kind=kLoop, calls=%fused_computation.31.clone.1 | loop fusion | flops 7602160 | bytes 6373504 | tf_op jit(solution)/shard_map/while/body/eval_jaxpr/reduce_sum | solution.py:71
  313.2 4.5 %fusion.62 = f32[16,256,256]{2,1,0:T(8,128)} fusion(bf16[12,16,128,128]{2,3,1,0:T(8,128)(2,1)} %get-tuple-element.403, s32[]{:T(128)} %get-tuple-element.390, bf16[128,256]{1,0:T(8,128)(2,1)S(1)} %get-tuple-element.405, bf16[256,128]{1,0:T(8,128)(2,1)S(1)} %get-tuple-element.404), kind=kOutput, calls=%fused_computation.10.clone.1 | convolution fusion | flops 403177472 | bytes 4850176 | tf_op jit(solution)/shard_map/while/body/eval_jaxpr/bfx,xk->bfk/dot_general | solution.py:129
  317.8 2.5 gather_fusion
  320.4 10.9 %add_reduce_fusion.2 = (f32[16]{0:T(128)S(1)}, f32[16,128,128]{2,1,0:T(8,128)S(1)}) fusion(f32[16,256,256]{2,1,0:T(8,128)} %fusion.62, bf16[16,2,128,128]{3,2,1,0:T(8,128)(2,1)S(1)} %gather_fusion, f32[16,128]{1,0:T(8,128)S(1)} %get-tuple-element.371, f32[16,128]{1,0:T(8,128)S(1)} %get-tuple-element.372, f32[128,128]{1,0:T(8,128)S(1)} %add_multiply_fusion.3, ...), kind=kLoop, calls=%fused_computation.31.clone.1 | loop fusion | flops 7602160 | bytes 6373504 | tf_op jit(solution)/shard_map/while/body/eval_jaxpr/reduce_sum | solution.py:71
  331.9 4.5 %fusion.62 = f32[16,256,256]{2,1,0:T(8,128)} fusion(bf16[12,16,128,128]{2,3,1,0:T(8,128)(2,1)} %get-tuple-element.403, s32[]{:T(128)} %get-tuple-element.390, bf16[128,256]{1,0:T(8,128)(2,1)S(1)} %get-tuple-element.405, bf16[256,128]{1,0:T(8,128)(2,1)S(1)} %get-tuple-element.404), kind=kOutput, calls=%fused_computation.10.clone.1 | convolution fusion | flops 403177472 | bytes 4850176 | tf_op jit(solution)/shard_map/while/body/eval_jaxpr/bfx,xk->bfk/dot_general | solution.py:129
  336.4 2.5 gather_fusion
  339.0 10.9 %add_reduce_fusion.2 = (f32[16]{0:T(128)S(1)}, f32[16,128,128]{2,1,0:T(8,128)S(1)}) fusion(f32[16,256,256]{2,1,0:T(8,128)} %fusion.62, bf16[16,2,128,128]{3,2,1,0:T(8,128)(2,1)S(1)} %gather_fusion, f32[16,128]{1,0:T(8,128)S(1)} %get-tuple-element.371, f32[16,128]{1,0:T(8,128)S(1)} %get-tuple-element.372, f32[128,128]{1,0:T(8,128)S(1)} %add_multiply_fusion.3, ...), kind=kLoop, calls=%fused_computation.31.clone.1 | loop fusion | flops 7602160 | bytes 6373504 | tf_op jit(solution)/shard_map/while/body/eval_jaxpr/reduce_sum | solution.py:71
  350.5 4.5 %fusion.62 = f32[16,256,256]{2,1,0:T(8,128)} fusion(bf16[12,16,128,128]{2,3,1,0:T(8,128)(2,1)} %get-tuple-element.403, s32[]{:T(128)} %get-tuple-element.390, bf16[128,256]{1,0:T(8,128)(2,1)S(1)} %get-tuple-element.405, bf16[256,128]{1,0:T(8,128)(2,1)S(1)} %get-tuple-element.404), kind=kOutput, calls=%fused_computation.10.clone.1 | convolution fusion | flops 403177472 | bytes 4850176 | tf_op jit(solution)/shard_map/while/body/eval_jaxpr/bfx,xk->bfk/dot_general | solution.py:129
  355.1 2.5 gather_fusion
  357.7 10.9 %add_reduce_fusion.2 = (f32[16]{0:T(128)S(1)}, f32[16,128,128]{2,1,0:T(8,128)S(1)}) fusion(f32[16,256,256]{2,1,0:T(8,128)} %fusion.62, bf16[16,2,128,128]{3,2,1,0:T(8,128)(2,1)S(1)} %gather_fusion, f32[16,128]{1,0:T(8,128)S(1)} %get-tuple-element.371, f32[16,128]{1,0:T(8,128)S(1)} %get-tuple-element.372, f32[128,128]{1,0:T(8,128)S(1)} %add_multiply_fusion.3, ...), kind=kLoop, calls=%fused_computation.31.clone.1 | loop fusion | flops 7602160 | bytes 6373504 | tf_op jit(solution)/shard_map/while/body/eval_jaxpr/reduce_sum | solution.py:71
  369.2 4.5 %fusion.62 = f32[16,256,256]{2,1,0:T(8,128)} fusion(bf16[12,16,128,128]{2,3,1,0:T(8,128)(2,1)} %get-tuple-element.403, s32[]{:T(128)} %get-tuple-element.390, bf16[128,256]{1,0:T(8,128)(2,1)S(1)} %get-tuple-element.405, bf16[256,128]{1,0:T(8,128)(2,1)S(1)} %get-tuple-element.404), kind=kOutput, calls=%fused_computation.10.clone.1 | convolution fusion | flops 403177472 | bytes 4850176 | tf_op jit(solution)/shard_map/while/body/eval_jaxpr/bfx,xk->bfk/dot_general | solution.py:129
  373.7 2.5 gather_fusion
  376.3 10.9 %add_reduce_fusion.2 = (f32[16]{0:T(128)S(1)}, f32[16,128,128]{2,1,0:T(8,128)S(1)}) fusion(f32[16,256,256]{2,1,0:T(8,128)} %fusion.62, bf16[16,2,128,128]{3,2,1,0:T(8,128)(2,1)S(1)} %gather_fusion, f32[16,128]{1,0:T(8,128)S(1)} %get-tuple-element.371, f32[16,128]{1,0:T(8,128)S(1)} %get-tuple-element.372, f32[128,128]{1,0:T(8,128)S(1)} %add_multiply_fusion.3, ...), kind=kLoop, calls=%fused_computation.31.clone.1 | loop fusion | flops 7602160 | bytes 6373504 | tf_op jit(solution)/shard_map/while/body/eval_jaxpr/reduce_sum | solution.py:71
  387.8 4.5 %fusion.62 = f32[16,256,256]{2,1,0:T(8,128)} fusion(bf16[12,16,128,128]{2,3,1,0:T(8,128)(2,1)} %get-tuple-element.403, s32[]{:T(128)} %get-tuple-element.390, bf16[128,256]{1,0:T(8,128)(2,1)S(1)} %get-tuple-element.405, bf16[256,128]{1,0:T(8,128)(2,1)S(1)} %get-tuple-element.404), kind=kOutput, calls=%fused_computation.10.clone.1 | convolution fusion | flops 403177472 | bytes 4850176 | tf_op jit(solution)/shard_map/while/body/eval_jaxpr/bfx,xk->bfk/dot_general | solution.py:129
  392.4 2.5 gather_fusion
  395.0 10.9 %add_reduce_fusion.2 = (f32[16]{0:T(128)S(1)}, f32[16,128,128]{2,1,0:T(8,128)S(1)}) fusion(f32[16,256,256]{2,1,0:T(8,128)} %fusion.62, bf16[16,2,128,128]{3,2,1,0:T(8,128)(2,1)S(1)} %gather_fusion, f32[16,128]{1,0:T(8,128)S(1)} %get-tuple-element.371, f32[16,128]{1,0:T(8,128)S(1)} %get-tuple-element.372, f32[128,128]{1,0:T(8,128)S(1)} %add_multiply_fusion.3, ...), kind=kLoop, calls=%fused_computation.31.clone.1 | loop fusion | flops 7602160 | bytes 6373504 | tf_op jit(solution)/shard_map/while/body/eval_jaxpr/reduce_sum | solution.py:71
  406.6 0.3 fusion.42
  406.9 26.7 %psum.6 = f32[10,2,256]{2,0,1:T(8,128)S(1)} all-reduce(f32[10,2,256]{2,0,1:T(8,128)S(1)} %fusion.42), channel_id=1, replica_groups=mesh['groups'=2,'dom'=8,'tilt'=2,'rep'=1] {'dom','rep'}, use_global_device_ids=true, to_apply=%region_12.13 | all-reduce | flops 5120 | bytes 40960 | tf_op jit(solution)/shard_map/psum | solution.py:175
  433.7 0.6 copy.111
  434.3 3.3 all-to-all-start.2
  437.6 0.6 copy.118
  438.3 4.9 %all-to-all-done.2 = f32[8,24,3]{1,2,0:T(4,128)S(1)} async-done(((f32[8,24,3]{1,2,0:T(4,128)}), f32[8,24,3]{1,2,0:T(4,128)S(1)}, u32[]{:S(2)}, u32[]{:S(2)}) %all-to-all-start.2) | async-done | bytes 2336 | tf_op jit(solution)/shard_map/all_to_all | solution.py:162
  443.3 0.6 gather_fusion.4
  444.0 0.6 copy.117
  (235 shorter events, 8.9 us)
Async XLA Ops:
  7.2 31.1 %all-to-all-start.1 = ((bf16[8,24,6]{1,2,0:T(8,128)(2,1)}), bf16[8,24,6]{1,2,0:T(8,128)(2,1)S(1)}, u32[]{:S(2)}, u32[]{:S(2)}) async-start(bf16[8,24,6]{1,2,0:T(8,128)(2,1)} %select_convert_fusion), calls=%async_computation.1 | async-start | bytes 32768 | tf_op jit(solution)/shard_map/all_to_all | solution.py:135
  38.3 6.1 %copy-start = (f32[10,2,256]{2,1,0:T(2,128)S(1)}, f32[10,2,256]{2,1,0:T(2,128)}, u32[]{:S(2)}) copy-start(f32[10,2,256]{2,1,0:T(2,128)} %param.15) | copy-start | bytes 61444
  38.3 144.3 %all-to-all-start = ((bf16[8,24,128,128]{2,3,1,0:T(8,128)(2,1)}), bf16[8,24,128,128]{2,3,1,0:T(8,128)(2,1)}, u32[]{:S(2)}, u32[]{:S(2)}) async-start(bf16[8,24,128,128]{2,3,1,0:T(8,128)(2,1)} %broadcast_select_fusion), calls=%async_computation | async-start | bytes 12582912 | tf_op jit(solution)/shard_map/all_to_all | solution.py:134
  434.3 8.9 %all-to-all-start.2 = ((f32[8,24,3]{1,2,0:T(4,128)}), f32[8,24,3]{1,2,0:T(4,128)S(1)}, u32[]{:S(2)}, u32[]{:S(2)}) async-start(f32[8,24,3]{1,2,0:T(4,128)} %copy.111), calls=%async_computation.2 | async-start | bytes 32768 | tf_op jit(solution)/shard_map/all_to_all | solution.py:162
where the time goes:
time: 447 us; the launch traced here: 445 us
  other arithmetic  149 us (33%)
  waiting for transfers between devices  141 us (32%)
  local copies, waits for them, and re-layouts  56.4 us (13%)
  matrix products  54.4 us (12%)
  blocking collectives  26.7 us (6%)
  starting transfers between devices  14.9 us (3%)
    all_to_all x1, waiting for transfers between devices, on_device(): lax.all_to_all(patch_buffer, 'dom', split_axis=0, concat_axis=0, tiled=True)  136 us
    reduce_sum x12, other arithmetic, spectral_terms(): jnp.sum(diff_real * diff_real + diff_imag * diff_imag, axis=(1, 2))  131 us
    dot_general x12, matrix products, one_block(): jnp.einsum('bfx,xk->bfk', first_pass, col_table, preferred_element_type=j...  54.1 us
    gather x12, local copies, waits for them, and re-layouts, one_block(): ref_blk = projected_flat[index_blk]  29.9 us
    psum x1, blocking collectives, on_device(): whole_grad = lax.psum(gradient, ('dom', 'rep'))  26.7 us
    gather x2, local copies, waits for them, and re-layouts, on_device(): patches[0][source]  18.8 us
  transfers between devices with their start and end apart: 3, of which 2 were waited for; matrix products, arithmetic and copies ran while one was open for 6% of the time, Pallas kernels for 0%

commit v1 on v0

--- a/solution.py
+++ b/solution.py
@@ -172,7 +172,7 @@
         precision=lax.Precision.HIGHEST,
         preferred_element_type=jnp.float32,
     ).reshape(tilt_dev, 2, node_count)
-    whole_grad = lax.psum(gradient, ("dom", "rep"))
+    whole_grad = lax.psum(lax.psum(gradient, "rep"), "dom")
     new_warp = warp_grid - whole_grad / jnp.sqrt(
         whole_grad * whole_grad + TRUST_FLOOR * TRUST_FLOOR
     )

time: 447 us -> 447 us (level)
  no operation moved by 1% of the time
where the time goes in v1:
time: 447 us; the launch traced here: 445 us
  other arithmetic  149 us (33%)
  waiting for transfers between devices  141 us (32%)
  local copies, waits for them, and re-layouts  56.4 us (13%)
  matrix products  54.4 us (12%)
  blocking collectives  26.7 us (6%)
  starting transfers between devices  14.9 us (3%)
    all_to_all x1, waiting for transfers between devices, on_device(): lax.all_to_all(patch_buffer, 'dom', split_axis=0, concat_axis=0, tiled=True)  136 us
    reduce_sum x12, other arithmetic, spectral_terms(): jnp.sum(diff_real * diff_real + diff_imag * diff_imag, axis=(1, 2))  131 us
    dot_general x12, matrix products, one_block(): jnp.einsum('bfx,xk->bfk', first_pass, col_table, preferred_element_type=j...  54.1 us
    gather x12, local copies, waits for them, and re-layouts, one_block(): ref_blk = projected_flat[index_blk]  29.9 us
    psum x1, blocking collectives, on_device(): whole_grad = lax.psum(lax.psum(gradient, 'rep'), 'dom')  26.7 us
    gather x2, local copies, waits for them, and re-layouts, on_device(): patches[0][source]  18.8 us
  transfers between devices with their start and end apart: 3, of which 2 were waited for; matrix products, arithmetic and copies ran while one was open for 6% of the time, Pallas kernels for 0%

profile of v1, /device:TPU:0, one launch (start us, length us, event | category | flops | bytes accessed | tf_op | source)
XLA Modules:
  0.0 444.6 jit_solution(1007006649997248516)
XLA Ops:
  0.6 0.7 and_select_fusion.2
  1.7 0.7 fusion.48
  2.4 0.7 multiply_add_fusion.1
  3.3 0.7 bitcast_convert_fusion
  4.1 0.7 convert_bitcast_fusion
  4.7 0.7 stack.8
  5.6 0.8 gather_fusion.2
  6.5 0.6 select_convert_fusion
  7.2 6.4 %all-to-all-start.1 = ((bf16[8,24,6]{1,2,0:T(8,128)(2,1)}), bf16[8,24,6]{1,2,0:T(8,128)(2,1)S(1)}, u32[]{:S(2)}, u32[]{:S(2)}) async-start(bf16[8,24,6]{1,2,0:T(8,128)(2,1)} %select_convert_fusion), calls=%async_computation.1 | async-start | bytes 32768 | tf_op jit(solution)/shard_map/all_to_all | solution.py:135
  13.5 10.2 %gather_fusion.1 = bf16[192,128,128]{2,1,0:T(8,128)(2,1)} fusion(bf16[128,128,128]{2,1,0:T(8,128)(2,1)} %bitcast.181, s32[1024]{0:T(1024)S(1)} %pad_clamp_fusion.3), kind=kCustom, calls=%fused_computation.1 | custom fusion | bytes 12583680 | tf_op jit(solution)/shard_map/gather | solution.py:100
  23.8 8.6 %copy.103 = bf16[8,24,128,128]{2,3,1,0:T(8,128)(2,1)} copy(bf16[8,24,128,128]{3,2,1,0:T(8,128)(2,1)} %bitcast.179) | data formatting | bytes 12582912 | tf_op jit(solution)/shard_map/gather | solution.py:100
  32.4 5.9 %broadcast_select_fusion = bf16[8,24,128,128]{2,3,1,0:T(8,128)(2,1)} fusion(bf16[8,24,128,128]{2,3,1,0:T(8,128)(2,1)} %copy.103, pred[8,24]{1,0:T(8,128)(4,1)S(1)} %broadcast_in_dim.106), kind=kLoop, calls=%fused_computation.65 | loop fusion | flops 3145728 | bytes 12583104 | tf_op jit(solution)/shard_map/jit(_where)/select_n | solution.py:100
  38.3 5.2 %all-to-all-start = ((bf16[8,24,128,128]{2,3,1,0:T(8,128)(2,1)}), bf16[8,24,128,128]{2,3,1,0:T(8,128)(2,1)}, u32[]{:S(2)}, u32[]{:S(2)}) async-start(bf16[8,24,128,128]{2,3,1,0:T(8,128)(2,1)} %broadcast_select_fusion), calls=%async_computation | async-start | bytes 12582912 | tf_op jit(solution)/shard_map/all_to_all | solution.py:134
  44.4 1.1 gather_fusion.3
  46.3 136.3 %all-to-all-done = bf16[8,24,128,128]{2,3,1,0:T(8,128)(2,1)} async-done(((bf16[8,24,128,128]{2,3,1,0:T(8,128)(2,1)}), bf16[8,24,128,128]{2,3,1,0:T(8,128)(2,1)}, u32[]{:S(2)}, u32[]{:S(2)}) %all-to-all-start) | async-done | bytes 6291488 | tf_op jit(solution)/shard_map/all_to_all | solution.py:134
  182.6 223.7 %while.15 = (s32[]{:T(128)}, f32[12,16,3]{1,0,2:T(8,128)S(1)}, bf16[12,16,128,128]{2,3,1,0:T(8,128)(2,1)}, bf16[256,128]{1,0:T(8,128)(2,1)S(1)}, bf16[128,256]{1...) while((s32[]{:T(128)}, f32[12,16,3]{1,0,2:T(8,128)S(1)}, ...), condition=%wide.region_11.12_spmd.clone.clone, body=%wide.region_7.11_spmd.clone.clone.sunk | while | flops 411868064 | bytes 14461309 | solution.py:148
  182.7 4.5 %fusion.62 = f32[16,256,256]{2,1,0:T(8,128)} fusion(bf16[12,16,128,128]{2,3,1,0:T(8,128)(2,1)} %get-tuple-element.403, s32[]{:T(128)} %get-tuple-element.390, bf16[128,256]{1,0:T(8,128)(2,1)S(1)} %get-tuple-element.405, bf16[256,128]{1,0:T(8,128)(2,1)S(1)} %get-tuple-element.404), kind=kOutput, calls=%fused_computation.10.clone.1 | convolution fusion | flops 403177472 | bytes 4850176 | tf_op jit(solution)/shard_map/while/body/eval_jaxpr/bfx,xk->bfk/dot_general | solution.py:129
  187.2 2.5 gather_fusion
  189.8 10.9 %add_reduce_fusion.2 = (f32[16]{0:T(128)S(1)}, f32[16,128,128]{2,1,0:T(8,128)S(1)}) fusion(f32[16,256,256]{2,1,0:T(8,128)} %fusion.62, bf16[16,2,128,128]{3,2,1,0:T(8,128)(2,1)S(1)} %gather_fusion, f32[16,128]{1,0:T(8,128)S(1)} %get-tuple-element.371, f32[16,128]{1,0:T(8,128)S(1)} %get-tuple-element.372, f32[128,128]{1,0:T(8,128)S(1)} %add_multiply_fusion.3, ...), kind=kLoop, calls=%fused_computation.31.clone.1 | loop fusion | flops 7602160 | bytes 6373504 | tf_op jit(solution)/shard_map/while/body/eval_jaxpr/reduce_sum | solution.py:71
  200.8 0.3 multiply_reduce_fusion.4
  201.3 4.5 %fusion.62 = f32[16,256,256]{2,1,0:T(8,128)} fusion(bf16[12,16,128,128]{2,3,1,0:T(8,128)(2,1)} %get-tuple-element.403, s32[]{:T(128)} %get-tuple-element.390, bf16[128,256]{1,0:T(8,128)(2,1)S(1)} %get-tuple-element.405, bf16[256,128]{1,0:T(8,128)(2,1)S(1)} %get-tuple-element.404), kind=kOutput, calls=%fused_computation.10.clone.1 | convolution fusion | flops 403177472 | bytes 4850176 | tf_op jit(solution)/shard_map/while/body/eval_jaxpr/bfx,xk->bfk/dot_general | solution.py:129
  205.9 2.5 gather_fusion
  208.5 10.9 %add_reduce_fusion.2 = (f32[16]{0:T(128)S(1)}, f32[16,128,128]{2,1,0:T(8,128)S(1)}) fusion(f32[16,256,256]{2,1,0:T(8,128)} %fusion.62, bf16[16,2,128,128]{3,2,1,0:T(8,128)(2,1)S(1)} %gather_fusion, f32[16,128]{1,0:T(8,128)S(1)} %get-tuple-element.371, f32[16,128]{1,0:T(8,128)S(1)} %get-tuple-element.372, f32[128,128]{1,0:T(8,128)S(1)} %add_multiply_fusion.3, ...), kind=kLoop, calls=%fused_computation.31.clone.1 | loop fusion | flops 7602160 | bytes 6373504 | tf_op jit(solution)/shard_map/while/body/eval_jaxpr/reduce_sum | solution.py:71
  219.4 0.3 multiply_reduce_fusion.4
  220.0 4.5 %fusion.62 = f32[16,256,256]{2,1,0:T(8,128)} fusion(bf16[12,16,128,128]{2,3,1,0:T(8,128)(2,1)} %get-tuple-element.403, s32[]{:T(128)} %get-tuple-element.390, bf16[128,256]{1,0:T(8,128)(2,1)S(1)} %get-tuple-element.405, bf16[256,128]{1,0:T(8,128)(2,1)S(1)} %get-tuple-element.404), kind=kOutput, calls=%fused_computation.10.clone.1 | convolution fusion | flops 403177472 | bytes 4850176 | tf_op jit(solution)/shard_map/while/body/eval_jaxpr/bfx,xk->bfk/dot_general | solution.py:129
  224.5 2.5 gather_fusion
  227.1 10.9 %add_reduce_fusion.2 = (f32[16]{0:T(128)S(1)}, f32[16,128,128]{2,1,0:T(8,128)S(1)}) fusion(f32[16,256,256]{2,1,0:T(8,128)} %fusion.62, bf16[16,2,128,128]{3,2,1,0:T(8,128)(2,1)S(1)} %gather_fusion, f32[16,128]{1,0:T(8,128)S(1)} %get-tuple-element.371, f32[16,128]{1,0:T(8,128)S(1)} %get-tuple-element.372, f32[128,128]{1,0:T(8,128)S(1)} %add_multiply_fusion.3, ...), kind=kLoop, calls=%fused_computation.31.clone.1 | loop fusion | flops 7602160 | bytes 6373504 | tf_op jit(solution)/shard_map/while/body/eval_jaxpr/reduce_sum | solution.py:71
  238.1 0.3 multiply_reduce_fusion.4
  238.6 4.5 %fusion.62 = f32[16,256,256]{2,1,0:T(8,128)} fusion(bf16[12,16,128,128]{2,3,1,0:T(8,128)(2,1)} %get-tuple-element.403, s32[]{:T(128)} %get-tuple-element.390, bf16[128,256]{1,0:T(8,128)(2,1)S(1)} %get-tuple-element.405, bf16[256,128]{1,0:T(8,128)(2,1)S(1)} %get-tuple-element.404), kind=kOutput, calls=%fused_computation.10.clone.1 | convolution fusion | flops 403177472 | bytes 4850176 | tf_op jit(solution)/shard_map/while/body/eval_jaxpr/bfx,xk->bfk/dot_general | solution.py:129
  243.2 2.5 gather_fusion
  245.8 10.9 %add_reduce_fusion.2 = (f32[16]{0:T(128)S(1)}, f32[16,128,128]{2,1,0:T(8,128)S(1)}) fusion(f32[16,256,256]{2,1,0:T(8,128)} %fusion.62, bf16[16,2,128,128]{3,2,1,0:T(8,128)(2,1)S(1)} %gather_fusion, f32[16,128]{1,0:T(8,128)S(1)} %get-tuple-element.371, f32[16,128]{1,0:T(8,128)S(1)} %get-tuple-element.372, f32[128,128]{1,0:T(8,128)S(1)} %add_multiply_fusion.3, ...), kind=kLoop, calls=%fused_computation.31.clone.1 | loop fusion | flops 7602160 | bytes 6373504 | tf_op jit(solution)/shard_map/while/body/eval_jaxpr/reduce_sum | solution.py:71
  256.7 0.3 multiply_reduce_fusion.4
  257.3 4.5 %fusion.62 = f32[16,256,256]{2,1,0:T(8,128)} fusion(bf16[12,16,128,128]{2,3,1,0:T(8,128)(2,1)} %get-tuple-element.403, s32[]{:T(128)} %get-tuple-element.390, bf16[128,256]{1,0:T(8,128)(2,1)S(1)} %get-tuple-element.405, bf16[256,128]{1,0:T(8,128)(2,1)S(1)} %get-tuple-element.404), kind=kOutput, calls=%fused_computation.10.clone.1 | convolution fusion | flops 403177472 | bytes 4850176 | tf_op jit(solution)/shard_map/while/body/eval_jaxpr/bfx,xk->bfk/dot_general | solution.py:129
  261.8 2.5 gather_fusion
  264.4 10.9 %add_reduce_fusion.2 = (f32[16]{0:T(128)S(1)}, f32[16,128,128]{2,1,0:T(8,128)S(1)}) fusion(f32[16,256,256]{2,1,0:T(8,128)} %fusion.62, bf16[16,2,128,128]{3,2,1,0:T(8,128)(2,1)S(1)} %gather_fusion, f32[16,128]{1,0:T(8,128)S(1)} %get-tuple-element.371, f32[16,128]{1,0:T(8,128)S(1)} %get-tuple-element.372, f32[128,128]{1,0:T(8,128)S(1)} %add_multiply_fusion.3, ...), kind=kLoop, calls=%fused_computation.31.clone.1 | loop fusion | flops 7602160 | bytes 6373504 | tf_op jit(solution)/shard_map/while/body/eval_jaxpr/reduce_sum | solution.py:71
  275.9 4.5 %fusion.62 = f32[16,256,256]{2,1,0:T(8,128)} fusion(bf16[12,16,128,128]{2,3,1,0:T(8,128)(2,1)} %get-tuple-element.403, s32[]{:T(128)} %get-tuple-element.390, bf16[128,256]{1,0:T(8,128)(2,1)S(1)} %get-tuple-element.405, bf16[256,128]{1,0:T(8,128)(2,1)S(1)} %get-tuple-element.404), kind=kOutput, calls=%fused_computation.10.clone.1 | convolution fusion | flops 403177472 | bytes 4850176 | tf_op jit(solution)/shard_map/while/body/eval_jaxpr/bfx,xk->bfk/dot_general | solution.py:129
  280.5 2.5 gather_fusion
  283.1 10.9 %add_reduce_fusion.2 = (f32[16]{0:T(128)S(1)}, f32[16,128,128]{2,1,0:T(8,128)S(1)}) fusion(f32[16,256,256]{2,1,0:T(8,128)} %fusion.62, bf16[16,2,128,128]{3,2,1,0:T(8,128)(2,1)S(1)} %gather_fusion, f32[16,128]{1,0:T(8,128)S(1)} %get-tuple-element.371, f32[16,128]{1,0:T(8,128)S(1)} %get-tuple-element.372, f32[128,128]{1,0:T(8,128)S(1)} %add_multiply_fusion.3, ...), kind=kLoop, calls=%fused_computation.31.clone.1 | loop fusion | flops 7602160 | bytes 6373504 | tf_op jit(solution)/shard_map/while/body/eval_jaxpr/reduce_sum | solution.py:71
  294.6 4.5 %fusion.62 = f32[16,256,256]{2,1,0:T(8,128)} fusion(bf16[12,16,128,128]{2,3,1,0:T(8,128)(2,1)} %get-tuple-element.403, s32[]{:T(128)} %get-tuple-element.390, bf16[128,256]{1,0:T(8,128)(2,1)S(1)} %get-tuple-element.405, bf16[256,128]{1,0:T(8,128)(2,1)S(1)} %get-tuple-element.404), kind=kOutput, calls=%fused_computation.10.clone.1 | convolution fusion | flops 403177472 | bytes 4850176 | tf_op jit(solution)/shard_map/while/body/eval_jaxpr/bfx,xk->bfk/dot_general | solution.py:129
  299.1 2.5 gather_fusion
  301.7 10.9 %add_reduce_fusion.2 = (f32[16]{0:T(128)S(1)}, f32[16,128,128]{2,1,0:T(8,128)S(1)}) fusion(f32[16,256,256]{2,1,0:T(8,128)} %fusion.62, bf16[16,2,128,128]{3,2,1,0:T(8,128)(2,1)S(1)} %gather_fusion, f32[16,128]{1,0:T(8,128)S(1)} %get-tuple-element.371, f32[16,128]{1,0:T(8,128)S(1)} %get-tuple-element.372, f32[128,128]{1,0:T(8,128)S(1)} %add_multiply_fusion.3, ...), kind=kLoop, calls=%fused_computation.31.clone.1 | loop fusion | flops 7602160 | bytes 6373504 | tf_op jit(solution)/shard_map/while/body/eval_jaxpr/reduce_sum | solution.py:71
  313.2 4.5 %fusion.62 = f32[16,256,256]{2,1,0:T(8,128)} fusion(bf16[12,16,128,128]{2,3,1,0:T(8,128)(2,1)} %get-tuple-element.403, s32[]{:T(128)} %get-tuple-element.390, bf16[128,256]{1,0:T(8,128)(2,1)S(1)} %get-tuple-element.405, bf16[256,128]{1,0:T(8,128)(2,1)S(1)} %get-tuple-element.404), kind=kOutput, calls=%fused_computation.10.clone.1 | convolution fusion | flops 403177472 | bytes 4850176 | tf_op jit(solution)/shard_map/while/body/eval_jaxpr/bfx,xk->bfk/dot_general | solution.py:129
  317.8 2.5 gather_fusion
  320.4 10.9 %add_reduce_fusion.2 = (f32[16]{0:T(128)S(1)}, f32[16,128,128]{2,1,0:T(8,128)S(1)}) fusion(f32[16,256,256]{2,1,0:T(8,128)} %fusion.62, bf16[16,2,128,128]{3,2,1,0:T(8,128)(2,1)S(1)} %gather_fusion, f32[16,128]{1,0:T(8,128)S(1)} %get-tuple-element.371, f32[16,128]{1,0:T(8,128)S(1)} %get-tuple-element.372, f32[128,128]{1,0:T(8,128)S(1)} %add_multiply_fusion.3, ...), kind=kLoop, calls=%fused_computation.31.clone.1 | loop fusion | flops 7602160 | bytes 6373504 | tf_op jit(solution)/shard_map/while/body/eval_jaxpr/reduce_sum | solution.py:71
  331.9 4.5 %fusion.62 = f32[16,256,256]{2,1,0:T(8,128)} fusion(bf16[12,16,128,128]{2,3,1,0:T(8,128)(2,1)} %get-tuple-element.403, s32[]{:T(128)} %get-tuple-element.390, bf16[128,256]{1,0:T(8,128)(2,1)S(1)} %get-tuple-element.405, bf16[256,128]{1,0:T(8,128)(2,1)S(1)} %get-tuple-element.404), kind=kOutput, calls=%fused_computation.10.clone.1 | convolution fusion | flops 403177472 | bytes 4850176 | tf_op jit(solution)/shard_map/while/body/eval_jaxpr/bfx,xk->bfk/dot_general | solution.py:129
  336.4 2.5 gather_fusion
  339.0 10.9 %add_reduce_fusion.2 = (f32[16]{0:T(128)S(1)}, f32[16,128,128]{2,1,0:T(8,128)S(1)}) fusion(f32[16,256,256]{2,1,0:T(8,128)} %fusion.62, bf16[16,2,128,128]{3,2,1,0:T(8,128)(2,1)S(1)} %gather_fusion, f32[16,128]{1,0:T(8,128)S(1)} %get-tuple-element.371, f32[16,128]{1,0:T(8,128)S(1)} %get-tuple-element.372, f32[128,128]{1,0:T(8,128)S(1)} %add_multiply_fusion.3, ...), kind=kLoop, calls=%fused_computation.31.clone.1 | loop fusion | flops 7602160 | bytes 6373504 | tf_op jit(solution)/shard_map/while/body/eval_jaxpr/reduce_sum | solution.py:71
  350.5 4.5 %fusion.62 = f32[16,256,256]{2,1,0:T(8,128)} fusion(bf16[12,16,128,128]{2,3,1,0:T(8,128)(2,1)} %get-tuple-element.403, s32[]{:T(128)} %get-tuple-element.390, bf16[128,256]{1,0:T(8,128)(2,1)S(1)} %get-tuple-element.405, bf16[256,128]{1,0:T(8,128)(2,1)S(1)} %get-tuple-element.404), kind=kOutput, calls=%fused_computation.10.clone.1 | convolution fusion | flops 403177472 | bytes 4850176 | tf_op jit(solution)/shard_map/while/body/eval_jaxpr/bfx,xk->bfk/dot_general | solution.py:129
  355.1 2.5 gather_fusion
  357.7 10.9 %add_reduce_fusion.2 = (f32[16]{0:T(128)S(1)}, f32[16,128,128]{2,1,0:T(8,128)S(1)}) fusion(f32[16,256,256]{2,1,0:T(8,128)} %fusion.62, bf16[16,2,128,128]{3,2,1,0:T(8,128)(2,1)S(1)} %gather_fusion, f32[16,128]{1,0:T(8,128)S(1)} %get-tuple-element.371, f32[16,128]{1,0:T(8,128)S(1)} %get-tuple-element.372, f32[128,128]{1,0:T(8,128)S(1)} %add_multiply_fusion.3, ...), kind=kLoop, calls=%fused_computation.31.clone.1 | loop fusion | flops 7602160 | bytes 6373504 | tf_op jit(solution)/shard_map/while/body/eval_jaxpr/reduce_sum | solution.py:71
  369.2 4.5 %fusion.62 = f32[16,256,256]{2,1,0:T(8,128)} fusion(bf16[12,16,128,128]{2,3,1,0:T(8,128)(2,1)} %get-tuple-element.403, s32[]{:T(128)} %get-tuple-element.390, bf16[128,256]{1,0:T(8,128)(2,1)S(1)} %get-tuple-element.405, bf16[256,128]{1,0:T(8,128)(2,1)S(1)} %get-tuple-element.404), kind=kOutput, calls=%fused_computation.10.clone.1 | convolution fusion | flops 403177472 | bytes 4850176 | tf_op jit(solution)/shard_map/while/body/eval_jaxpr/bfx,xk->bfk/dot_general | solution.py:129
  373.7 2.5 gather_fusion
  376.3 10.9 %add_reduce_fusion.2 = (f32[16]{0:T(128)S(1)}, f32[16,128,128]{2,1,0:T(8,128)S(1)}) fusion(f32[16,256,256]{2,1,0:T(8,128)} %fusion.62, bf16[16,2,128,128]{3,2,1,0:T(8,128)(2,1)S(1)} %gather_fusion, f32[16,128]{1,0:T(8,128)S(1)} %get-tuple-element.371, f32[16,128]{1,0:T(8,128)S(1)} %get-tuple-element.372, f32[128,128]{1,0:T(8,128)S(1)} %add_multiply_fusion.3, ...), kind=kLoop, calls=%fused_computation.31.clone.1 | loop fusion | flops 7602160 | bytes 6373504 | tf_op jit(solution)/shard_map/while/body/eval_jaxpr/reduce_sum | solution.py:71
  387.8 4.5 %fusion.62 = f32[16,256,256]{2,1,0:T(8,128)} fusion(bf16[12,16,128,128]{2,3,1,0:T(8,128)(2,1)} %get-tuple-element.403, s32[]{:T(128)} %get-tuple-element.390, bf16[128,256]{1,0:T(8,128)(2,1)S(1)} %get-tuple-element.405, bf16[256,128]{1,0:T(8,128)(2,1)S(1)} %get-tuple-element.404), kind=kOutput, calls=%fused_computation.10.clone.1 | convolution fusion | flops 403177472 | bytes 4850176 | tf_op jit(solution)/shard_map/while/body/eval_jaxpr/bfx,xk->bfk/dot_general | solution.py:129
  392.4 2.5 gather_fusion
  395.0 10.9 %add_reduce_fusion.2 = (f32[16]{0:T(128)S(1)}, f32[16,128,128]{2,1,0:T(8,128)S(1)}) fusion(f32[16,256,256]{2,1,0:T(8,128)} %fusion.62, bf16[16,2,128,128]{3,2,1,0:T(8,128)(2,1)S(1)} %gather_fusion, f32[16,128]{1,0:T(8,128)S(1)} %get-tuple-element.371, f32[16,128]{1,0:T(8,128)S(1)} %get-tuple-element.372, f32[128,128]{1,0:T(8,128)S(1)} %add_multiply_fusion.3, ...), kind=kLoop, calls=%fused_computation.31.clone.1 | loop fusion | flops 7602160 | bytes 6373504 | tf_op jit(solution)/shard_map/while/body/eval_jaxpr/reduce_sum | solution.py:71
  406.6 0.3 fusion.42
  406.9 26.7 %psum.6 = f32[10,2,256]{2,0,1:T(8,128)S(1)} all-reduce(f32[10,2,256]{2,0,1:T(8,128)S(1)} %fusion.42), channel_id=1, replica_groups=mesh['groups'=2,'dom'=8,'tilt'=2,'rep'=1] {'dom'}, use_global_device_ids=true, to_apply=%region_12.13 | all-reduce | flops 5120 | bytes 40960 | tf_op jit(solution)/shard_map/psum | solution.py:175
  433.7 0.6 copy.111
  434.3 3.3 all-to-all-start.2
  437.6 0.6 copy.118
  438.3 4.9 %all-to-all-done.2 = f32[8,24,3]{1,2,0:T(4,128)S(1)} async-done(((f32[8,24,3]{1,2,0:T(4,128)}), f32[8,24,3]{1,2,0:T(4,128)S(1)}, u32[]{:S(2)}, u32[]{:S(2)}) %all-to-all-start.2) | async-done | bytes 2336 | tf_op jit(solution)/shard_map/all_to_all | solution.py:162
  443.3 0.6 gather_fusion.4
  444.0 0.6 copy.117
  (235 shorter events, 8.9 us)
Async XLA Ops:
  7.2 31.1 %all-to-all-start.1 = ((bf16[8,24,6]{1,2,0:T(8,128)(2,1)}), bf16[8,24,6]{1,2,0:T(8,128)(2,1)S(1)}, u32[]{:S(2)}, u32[]{:S(2)}) async-start(bf16[8,24,6]{1,2,0:T(8,128)(2,1)} %select_convert_fusion), calls=%async_computation.1 | async-start | bytes 32768 | tf_op jit(solution)/shard_map/all_to_all | solution.py:135
  38.3 6.1 %copy-start = (f32[10,2,256]{2,1,0:T(2,128)S(1)}, f32[10,2,256]{2,1,0:T(2,128)}, u32[]{:S(2)}) copy-start(f32[10,2,256]{2,1,0:T(2,128)} %param.15) | copy-start | bytes 61444
  38.3 144.3 %all-to-all-start = ((bf16[8,24,128,128]{2,3,1,0:T(8,128)(2,1)}), bf16[8,24,128,128]{2,3,1,0:T(8,128)(2,1)}, u32[]{:S(2)}, u32[]{:S(2)}) async-start(bf16[8,24,128,128]{2,3,1,0:T(8,128)(2,1)} %broadcast_select_fusion), calls=%async_computation | async-start | bytes 12582912 | tf_op jit(solution)/shard_map/all_to_all | solution.py:134
  434.3 8.9 %all-to-all-start.2 = ((f32[8,24,3]{1,2,0:T(4,128)}), f32[8,24,3]{1,2,0:T(4,128)S(1)}, u32[]{:S(2)}, u32[]{:S(2)}) async-start(f32[8,24,3]{1,2,0:T(4,128)} %copy.111), calls=%async_computation.2 | async-start | bytes 32768 | tf_op jit(solution)/shard_map/all_to_all | solution.py:162
